TPU v7x, 32 devices: a whole 2x2x4 slice. The times are simulated.
32 devices in a mesh: row: 4 (over z), col: 8 (over y, x, core).
Axes of the slice: x: 2, y: 2, z: 4, core: 2. Of those that a mesh axis runs over, the one named last changes fastest.
Arguments:
- src_field: bfloat16 [64, 1048576], P(None, ('row', 'col')), may hold values from 0.5 to 2
- src_area: float32 [1048576], P(('row', 'col')), may hold values from 0.3 to 3
- tgt_area: float32 [262144], P(('row', 'col')), may hold values from 0.3 to 3
- weights: bfloat16 [12288, 128, 128], P(('row', 'col')), may hold values from 0 to 0.0025939941
- send_index: int32 [32, 32, 2], P(('row', 'col')), may hold values from -1 to 255, as said below
- pair_slot: int32 [12288], P(('row', 'col')), may hold values from 0 to 63, as said below
- pair_target: int32 [12288], P(('row', 'col')), may hold values from 0 to 63, as said below
Outputs:
- target_field: float32 [64, 262144], P(None, ('row', 'col'))
Inputs may be any that keep to these rules, and one draw needn't show every extreme that they name: `send_index`: in each [s, r] the live entries (not -1) come first and there are 1 to 2 of them; every sender sends to every receiver; for each receiver some sender fills all 2 slots. `pair_slot`: each pair of device r names a live slot of what device r receives; every live slot is named by some pair of device r. `pair_target`: every local target block of a device is named by some pair of that device.
All inputs are finite; a program needn't handle non-finite values.
Results may differ from a plain program's by a relative error of at most 0.0003.
Values may be sent and summed in bfloat16 or wider, within the bound.
A program may use at most 128 MiB of HBM per device.

v0:
```python
import jax
import jax.numpy as jnp
from jax import lax
from jax.sharding import PartitionSpec as P


def shards(src_field, src_area, tgt_area, weights, send_index, pair_slot, pair_target):
    columns, cell_count = src_field.shape
    block_size = weights.shape[1]
    local_blocks = cell_count // block_size
    target_blocks = tgt_area.shape[0] // block_size
    send_rows = send_index[0]
    peer_count, capacity = send_rows.shape
    blocks = src_field.reshape(columns, local_blocks, block_size)
    source_local = jnp.sum(src_field.astype(jnp.float32) * src_area[None, :], axis=1)
    chosen = jnp.maximum(send_rows.reshape(-1), 0)
    outbound = jnp.take(blocks, chosen, axis=1)
    outbound = jnp.transpose(outbound, (1, 0, 2)).reshape(peer_count, capacity, columns, block_size)
    inbound = lax.all_to_all(outbound, ("row", "col"), split_axis=0, concat_axis=0, tiled=True)
    inbound = inbound.reshape(peer_count * capacity, columns, block_size)
    picked = jnp.take(inbound, pair_slot, axis=0)
    products = jnp.einsum("pcs,pst->pct", picked, weights, preferred_element_type=jnp.float32)
    placed = jax.ops.segment_sum(products, pair_target, num_segments=target_blocks)
    regridded = jnp.transpose(placed, (1, 0, 2)).reshape(columns, target_blocks * block_size)
    target_local = jnp.sum(regridded * tgt_area[None, :], axis=1)
    source_mass, target_mass = lax.psum((source_local, target_local), ("row", "col"))
    return regridded * (source_mass / target_mass)[:, None]


def solution(mesh):
    in_specs = (
        P(None, ("row", "col")),
        P(("row", "col")),
        P(("row", "col")),
        P(("row", "col"), None, None),
        P(("row", "col"), None, None),
        P(("row", "col")),
        P(("row", "col")),
    )
    out_specs = P(None, ("row", "col"))
    return jax.shard_map(shards, mesh=mesh, in_specs=in_specs, out_specs=out_specs, check_vma=False)
```

profile of v0, /device:TPU:0, one launch (start us, length us, event | category | flops | bytes accessed | tf_op | source)
XLA Modules:
  0.0 152.7 jit_solution(11296800883933631301)
XLA Ops:
  0.0 0.7 broadcast_maximum_fusion
  0.7 0.7 broadcast_compare_fusion
  1.4 5.3 %copy_bitcast_fusion = bf16[64,256,128]{2,0,1:T(8,128)(2,1)} fusion(bf16[64,32768]{1,0:T(8,128)(2,1)} %param.7), kind=kLoop, calls=%fused_computation.7 | loop fusion | bytes 8388608 | tf_op jit(solution)/shard_map/reshape | solution.py:14
  6.7 0.0 copy-start.2
  6.7 0.0 copy-start
  6.7 0.1 copy.13
  6.8 0.1 reshape.53
  6.9 0.1 copy.12
  7.0 0.1 le.27
  7.1 2.9 %gather_fusion = bf16[64,64,128]{2,1,0:T(8,128)(2,1)S(1)} fusion(bf16[64,256,128]{2,0,1:T(8,128)(2,1)} %copy_bitcast_fusion, s32[1024]{0:T(1024)S(1)} %pad_clamp_fusion.1), kind=kCustom, calls=%fused_computation | custom fusion | bytes 2097408 | tf_op jit(solution)/shard_map/jit(_take)/gather | solution.py:17
  10.1 1.1 broadcast_select_fusion
  11.2 7.3 %all-to-all-start = ((bf16[32,2,64,128]{3,2,1,0:T(8,128)(2,1)}), bf16[32,2,64,128]{3,2,1,0:T(8,128)(2,1)S(1)}, u32[]{:S(2)}, u32[]{:S(2)}) async-start(bf16[32,2,64,128]{3,2,1,0:T(8,128)(2,1)} %bitcast), calls=%async_computation | async-start | bytes 2097152 | tf_op jit(solution)/shard_map/all_to_all | solution.py:19
  18.5 0.0 copy-done.2
  18.6 0.0 copy-done
  18.6 3.1 %multiply_reduce_fusion = f32[64]{0:T(128)S(1)} fusion(bf16[64,32768]{1,0:T(8,128)(2,1)} %param.7, f32[32768]{0:T(1024)S(1)} %copy-done), kind=kLoop, calls=%fused_computation.3 | loop fusion | flops 6291392 | bytes 4325632 | tf_op jit(solution)/shard_map/reduce_sum | solution.py:15
  21.7 23.0 %all-to-all-done = bf16[32,2,64,128]{3,2,1,0:T(8,128)(2,1)S(1)} async-done(((bf16[32,2,64,128]{3,2,1,0:T(8,128)(2,1)}), bf16[32,2,64,128]{3,2,1,0:T(8,128)(2,1)S(1)}, u32[]{:S(2)}, u32[]{:S(2)}) %all-to-all-start) | async-done | bytes 1048608 | tf_op jit(solution)/shard_map/all_to_all | solution.py:19
  44.7 13.3 %gather_fusion.1 = bf16[384,64,128]{2,1,0:T(8,128)(2,1)} fusion(bf16[64,64,128]{2,1,0:T(8,128)(2,1)S(1)} %bitcast.18, s32[1024]{0:T(1024)S(1)} %pad_clamp_fusion), kind=kCustom, calls=%fused_computation.1 | custom fusion | bytes 12584448 | tf_op jit(solution)/shard_map/jit(_take)/gather | solution.py:21
  58.1 0.0 copy-start.3
  58.1 14.4 %fusion = f32[384,64,128]{2,1,0:T(8,128)} fusion(bf16[384,128,128]{2,1,0:T(8,128)(2,1)} %param.10, bf16[384,64,128]{2,1,0:T(8,128)(2,1)} %gather_fusion.1, pred[384]{0:T(512)(128)(4,1)S(1)} %compare_and_fusion), kind=kOutput, calls=%fused_computation.4 | convolution fusion | flops 808452096 | bytes 31457664 | tf_op jit(solution)/shard_map/pcs,pst->pct/dot_general | solution.py:22
  72.5 0.2 broadcast_in_dim.31
  72.8 0.0 copy-done.3
  72.8 0.0 copy-start.1
  72.8 39.5 %scatter_fusion = f32[64,64,128]{2,1,0:T(8,128)S(1)} fusion(f32[64,64,128]{2,1,0:T(8,128)S(1)} %broadcast_in_dim.31, s32[384]{0:T(512)S(1)} %copy-done.3, f32[384,64,128]{2,1,0:T(8,128)} %fusion), kind=kCustom, calls=%fused_computation.2 | custom fusion | flops 3145728 | bytes 37750272 | tf_op jit(solution)/shard_map/scatter-add | solution.py:23
  112.3 0.0 copy-done.1
  112.3 0.3 fusion.4
  112.6 38.6 %all-reduce = (f32[64]{0:T(128)S(1)}, f32[64]{0:T(128)S(1)}) all-reduce(f32[64]{0:T(128)S(1)} %multiply_reduce_fusion, f32[64]{0:T(128)S(1)} %fusion.4), channel_id=1, replica_groups=mesh['row'=4,'col'=8] {'row','col'}, use_global_device_ids=true, to_apply=%region_2.3 | all-reduce | flops 128 | bytes 1024 | tf_op jit(solution)/shard_map/psum | solution.py:26
  151.1 1.5 %bitcast_multiply_fusion = f32[64,8192]{1,0:T(8,128)} fusion(f32[64]{0:T(128)S(1)} %div.3, f32[64,64,128]{2,1,0:T(8,128)S(1)} %scatter_fusion), kind=kLoop, calls=%fused_computation.9 | loop fusion | flops 524288 | bytes 4194560 | tf_op jit(solution)/shard_map/mul | solution.py:27
  (5 shorter events, 0.0 us)
Async XLA Ops:
  6.7 11.9 %copy-start.2 = (s32[384]{0:T(512)S(1)}, s32[384]{0:T(512)}, u32[]{:S(2)}) copy-start(s32[384]{0:T(512)} %param.12) | copy-start | bytes 4612
  6.7 11.9 %copy-start = (f32[32768]{0:T(1024)S(1)}, f32[32768]{0:T(1024)}, u32[]{:S(2)}) copy-start(f32[32768]{0:T(1024)} %param.8) | copy-start | bytes 393220
  11.2 33.5 %all-to-all-start = ((bf16[32,2,64,128]{3,2,1,0:T(8,128)(2,1)}), bf16[32,2,64,128]{3,2,1,0:T(8,128)(2,1)S(1)}, u32[]{:S(2)}, u32[]{:S(2)}) async-start(bf16[32,2,64,128]{3,2,1,0:T(8,128)(2,1)} %bitcast), calls=%async_computation | async-start | bytes 2097152 | tf_op jit(solution)/shard_map/all_to_all | solution.py:19
  58.1 14.7 %copy-start.3 = (s32[384]{0:T(512)S(1)}, s32[384]{0:T(512)}, u32[]{:S(2)}) copy-start(s32[384]{0:T(512)} %param.13) | copy-start | bytes 4612
  72.8 39.5 %copy-start.1 = (f32[8192]{0:T(1024)S(1)}, f32[8192]{0:T(1024)}, u32[]{:S(2)}) copy-start(f32[8192]{0:T(1024)} %param.9) | copy-start | bytes 98308
where the time goes:
time: 154 us; the launch traced here: 153 us
  other arithmetic  46.9 us (30%)
  blocking collectives  38.6 us (25%)
  waiting for transfers between devices  23 us (15%)
  local copies, waits for them, and re-layouts  22.3 us (14%)
  matrix products  14.4 us (9%)
  starting transfers between devices  7.33 us (5%)
    scatter-add x1, other arithmetic, shards(): jax.ops.segment_sum(products, pair_target, num_segments=target_blocks)  39.5 us
    psum x1, blocking collectives, shards(): lax.psum((source_local, target_local), ('row', 'col'))  38.6 us
    all_to_all x1, waiting for transfers between devices, shards(): lax.all_to_all(outbound, ('row', 'col'), split_axis=0, concat_axis=0, til...  23 us
    dot_general x1, matrix products, shards(): jnp.einsum('pcs,pst->pct', picked, weights, preferred_element_type=jnp.fl...  14.4 us
    gather x1, local copies, waits for them, and re-layouts, shards(): picked = jnp.take(inbound, pair_slot, axis=0)  13.3 us
    all_to_all x1, starting transfers between devices, shards(): lax.all_to_all(outbound, ('row', 'col'), split_axis=0, concat_axis=0, til...  7.33 us
    reshape x1, local copies, waits for them, and re-layouts, shards(): blocks = src_field.reshape(columns, local_blocks, block_size)  5.32 us
    reduce_sum x1, other arithmetic, shards(): jnp.sum(src_field.astype(jnp.float32) * src_area[None, :], axis=1)  3.1 us
  transfers between devices with their start and end apart: 1, of which 1 were waited for; matrix products, arithmetic and copies ran while one was open for 2% of the time, Pallas kernels for 0%

commit v1 on v0

v1 whole, which is shorter than its diff:
```python
import functools

import jax
import jax.numpy as jnp
from jax import lax
from jax.experimental import pallas as pl
from jax.experimental.pallas import tpu as pltpu
from jax.sharding import PartitionSpec as P

MESH = pl.DeviceIdType.MESH
LANES = 128


def lanes_of(column):
    total = jnp.sum(column, axis=1, keepdims=True)
    rows = lax.broadcasted_iota(jnp.int32, column.shape, 0)
    lanes = lax.broadcasted_iota(jnp.int32, column.shape, 1)
    return jnp.sum(jnp.where(rows == lanes, total, 0.0), axis=0, keepdims=True)


def place(cols):
    me = lax.axis_index("row") * cols + lax.axis_index("col")
    return me


def greet(n, cols, me):
    barrier = pltpu.get_barrier_semaphore()

    def hello(step, carry):
        peer = lax.rem(me + step, n)
        pl.semaphore_signal(barrier, inc=1, device_id=(peer // cols, lax.rem(peer, cols)), device_id_type=MESH)
        return carry

    lax.fori_loop(1, n, hello, 0)
    return barrier


def exchange_kernel(n, cols, send_ref, area_ref, src_ref, inbound_ref, mass_ref, src, outbound, load_sem, keep_sem, send_sem, recv_sem):
    me = place(cols)
    capacity, columns, block = outbound.shape[1:]

    def load(index, carry):
        cells = pl.ds(pl.multiple_of(index * block, block), block)
        pltpu.make_async_copy(src_ref.at[:, cells], src.at[index], load_sem).start()
        return carry

    lax.fori_loop(0, src.shape[0], load, 0, unroll=8)
    barrier = greet(n, cols, me)
    pltpu.make_async_copy(src, src, load_sem).wait()

    def gather(peer, carry):
        for slot in range(capacity):
            pick = jnp.maximum(send_ref[peer * capacity + slot], 0)
            outbound[peer, slot] = src[pick]
        return carry

    lax.fori_loop(0, n, gather, 0)
    pl.semaphore_wait(barrier, n - 1)

    def copy_to(step):
        peer = lax.rem(me + step, n)
        return pltpu.make_async_remote_copy(
            src_ref=outbound.at[peer],
            dst_ref=inbound_ref.at[me],
            send_sem=send_sem.at[step],
            recv_sem=recv_sem.at[step],
            device_id=(peer // cols, lax.rem(peer, cols)),
            device_id_type=MESH,
        )

    def send(step, carry):
        copy_to(step).start()
        return carry

    lax.fori_loop(1, n, send, 0)
    keep = pltpu.make_async_copy(outbound.at[me], inbound_ref.at[me], keep_sem)
    keep.start()

    def add(step, total):
        return total + src[step].astype(jnp.float32) * area_ref[pl.ds(step, 1), :]

    total = lax.fori_loop(0, area_ref.shape[0], add, jnp.zeros((columns, block), jnp.float32), unroll=8)
    mass_ref[...] = jnp.broadcast_to(lanes_of(total), mass_ref.shape)
    keep.wait()

    def finish(step, carry):
        copy_to(step).wait()
        return carry

    lax.fori_loop(1, n, finish, 0)


def exchange(n, cols, capacity, send_rows, area, src_field):
    columns, cells = src_field.shape
    block = area.shape[1]
    return pl.pallas_call(
        functools.partial(exchange_kernel, n, cols),
        out_shape=(
            jax.ShapeDtypeStruct((n, capacity, columns, block), jnp.bfloat16),
            jax.ShapeDtypeStruct((8, LANES), jnp.float32),
        ),
        in_specs=[
            pl.BlockSpec(memory_space=pltpu.SMEM),
            pl.BlockSpec(memory_space=pltpu.VMEM),
            pl.BlockSpec(memory_space=pl.ANY),
        ],
        out_specs=(pl.BlockSpec(memory_space=pl.ANY), pl.BlockSpec(memory_space=pltpu.VMEM)),
        scratch_shapes=[
            pltpu.VMEM((cells // block, columns, block), jnp.bfloat16),
            pltpu.VMEM((n, capacity, columns, block), jnp.bfloat16),
            pltpu.SemaphoreType.DMA,
            pltpu.SemaphoreType.DMA,
            pltpu.SemaphoreType.DMA((n,)),
            pltpu.SemaphoreType.DMA((n,)),
        ],
        compiler_params=pltpu.CompilerParams(collective_id=0, has_side_effects=True),
        name="exchange",
    )(send_rows, area, src_field)


def regrid_kernel(group, slot_ref, target_ref, inbound_ref, area_ref, weight_ref, out_ref, mass_ref):
    step = pl.program_id(0)
    pairs, block = weight_ref.shape[:2]
    columns = out_ref.shape[0]

    @pl.when(step == 0)
    def _():
        out_ref[...] = jnp.zeros_like(out_ref)

    @pl.loop(0, pairs // group)
    def _(outer):
        first = outer * group
        products = []
        for inner in range(group):
            slot = slot_ref[step * pairs + first + inner]
            products.append(jnp.dot(inbound_ref[slot], weight_ref[first + inner], preferred_element_type=jnp.float32))
        for inner in range(group):
            target = target_ref[step * pairs + first + inner]
            cells = pl.ds(pl.multiple_of(target * block, block), block)
            out_ref[:, cells] += products[inner]

    @pl.when(step == pl.num_programs(0) - 1)
    def _():
        def add(index, total):
            return total + out_ref[:, pl.ds(pl.multiple_of(index * block, block), block)] * area_ref[pl.ds(index, 1), :]

        total = lax.fori_loop(0, area_ref.shape[0], add, jnp.zeros((columns, block), jnp.float32), unroll=8)
        mass_ref[...] = jnp.broadcast_to(lanes_of(total), mass_ref.shape)


def regrid(inbound, area, weights, pair_slot, pair_target):
    slots, columns, block = inbound.shape
    pairs = weights.shape[0]
    targets = area.shape[0]
    step = 32
    whole = lambda *shape: pl.BlockSpec(shape, lambda i, *_: (0,) * len(shape))
    return pl.pallas_call(
        functools.partial(regrid_kernel, 4),
        out_shape=(
            jax.ShapeDtypeStruct((columns, targets * block), jnp.float32),
            jax.ShapeDtypeStruct((8, LANES), jnp.float32),
        ),
        grid_spec=pltpu.PrefetchScalarGridSpec(
            num_scalar_prefetch=2,
            grid=(pairs // step,),
            in_specs=[
                whole(slots, columns, block),
                whole(targets, block),
                pl.BlockSpec((step, block, block), lambda i, *_: (i, 0, 0)),
            ],
            out_specs=(whole(columns, targets * block), whole(8, LANES)),
        ),
        name="regrid",
    )(pair_slot, pair_target, inbound, area, weights)


def mass_kernel(n, cols, source_ref, target_ref, scale_ref, own, seen, send_sem, recv_sem):
    me = place(cols)
    barrier = greet(n, cols, me)
    rows = lax.broadcasted_iota(jnp.int32, own.shape, 0)
    own[...] = jnp.where(rows == 0, source_ref[...], target_ref[...])
    pl.semaphore_wait(barrier, n - 1)

    def copy_to(step):
        peer = lax.rem(me + step, n)
        return pltpu.make_async_remote_copy(
            src_ref=own,
            dst_ref=seen.at[step],
            send_sem=send_sem.at[step],
            recv_sem=recv_sem.at[step],
            device_id=(peer // cols, lax.rem(peer, cols)),
            device_id_type=MESH,
        )

    def send(step, carry):
        copy_to(step).start()
        return carry

    def finish(step, total):
        copy_to(step).wait()
        return total + seen[step]

    lax.fori_loop(1, n, send, 0)
    total = lax.fori_loop(1, n, finish, own[...])
    scale_ref[...] = jnp.broadcast_to(total[0:1] / total[1:2], scale_ref.shape)


def scales(n, cols, source, target):
    return pl.pallas_call(
        functools.partial(mass_kernel, n, cols),
        out_shape=jax.ShapeDtypeStruct((8, LANES), jnp.float32),
        in_specs=[pl.BlockSpec(memory_space=pltpu.VMEM)] * 2,
        out_specs=pl.BlockSpec(memory_space=pltpu.VMEM),
        scratch_shapes=[
            pltpu.VMEM((8, LANES), jnp.float32),
            pltpu.VMEM((n, 8, LANES), jnp.float32),
            pltpu.SemaphoreType.DMA((n,)),
            pltpu.SemaphoreType.DMA((n,)),
        ],
        compiler_params=pltpu.CompilerParams(collective_id=1, has_side_effects=True),
        name="masses",
    )(source, target)


def shards(n, cols, src_field, src_area, tgt_area, weights, send_index, pair_slot, pair_target):
    columns, cell_count = src_field.shape
    block = weights.shape[1]
    capacity = send_index.shape[2]
    inbound, source = exchange(n, cols, capacity, send_index.reshape(-1), src_area.reshape(-1, block), src_field)
    regridded, target = regrid(inbound.reshape(n * capacity, columns, block), tgt_area.reshape(-1, block), weights, pair_slot, pair_target)
    scale = scales(n, cols, source, target)
    return regridded * scale[0, :columns][:, None]


def solution(mesh):
    rows, cols = mesh.shape["row"], mesh.shape["col"]
    in_specs = (
        P(None, ("row", "col")),
        P(("row", "col")),
        P(("row", "col")),
        P(("row", "col"), None, None),
        P(("row", "col"), None, None),
        P(("row", "col")),
        P(("row", "col")),
    )
    out_specs = P(None, ("row", "col"))
    body = functools.partial(shards, rows * cols, cols)
    return jax.shard_map(body, mesh=mesh, in_specs=in_specs, out_specs=out_specs, check_vma=False)
```

time: 154 us -> 69.9 us (0.45)
  Pallas kernels: 0 us -> 64.4 us
  other arithmetic: 46.9 us -> 3.13 us
  blocking collectives: 38.6 us -> 0 us
  waiting for transfers between devices: 23 us -> 0 us
  local copies, waits for them, and re-layouts: 22.3 us -> 2.05 us
  matrix products: 14.4 us -> 0 us
  starting transfers between devices: 7.33 us -> 0 us
    pallas_call x0 -> x3, Pallas kernels: none -> 64.4 us  [the longest x1 27.2 us: exchange(): pl.pallas_call(functools.partial(exchange_kernel, n, cols), out_shape=(ja...]
    scatter-add x1 -> x0, other arithmetic: 39.5 us -> none  [shards(): jax.ops.segment_sum(products, pair_target, num_segments=target_blocks)]
    psum x1 -> x0, blocking collectives: 38.6 us -> none  [shards(): lax.psum((source_local, target_local), ('row', 'col'))]
    all_to_all x1 -> x0, waiting for transfers between devices: 23 us -> none  [shards(): lax.all_to_all(outbound, ('row', 'col'), split_axis=0, concat_axis=0, til...]
    gather x2 -> x0, local copies, waits for them, and re-layouts: 16.3 us -> none  [the longest x1 13.3 us: shards(): picked = jnp.take(inbound, pair_slot, axis=0)]
    dot_general x1 -> x0, matrix products: 14.4 us -> none  [shards(): jnp.einsum('pcs,pst->pct', picked, weights, preferred_element_type=jnp.fl...]
    all_to_all x1 -> x0, starting transfers between devices: 7.33 us -> none  [shards(): lax.all_to_all(outbound, ('row', 'col'), split_axis=0, concat_axis=0, til...]
    reshape x1, local copies, waits for them, and re-layouts: 5.32 us -> 0.62 us  [shards(): send_index.reshape(-1)]
  transfers between devices with their start and end apart: 1 -> 0, of which waited for: 1 -> 0; matrix products, arithmetic and copies ran while one was open for 2% -> 0% of each run, Pallas kernels for 0% -> 0%
where the time goes in v1:
time: 69.9 us; the launch traced here: 69.6 us
  Pallas kernels  64.4 us (92%)
  other arithmetic  3.13 us (4%)
  local copies, waits for them, and re-layouts  2.05 us (3%)
    pallas_call x1, Pallas kernels, exchange(): pl.pallas_call(functools.partial(exchange_kernel, n, cols), out_shape=(ja...  27.2 us
    pallas_call x1, Pallas kernels, regrid(): pl.pallas_call(functools.partial(regrid_kernel, 4), out_shape=(jax.ShapeD...  21 us
    pallas_call x1, Pallas kernels, scales(): pl.pallas_call(functools.partial(mass_kernel, n, cols), out_shape=jax.Sha...  16.1 us
    mul x1, other arithmetic, shards(): return regridded * scale[0, :columns][:, None]  3.13 us

profile of v1, /device:TPU:0, one launch (start us, length us, event | category | flops | bytes accessed | tf_op | source)
XLA Modules:
  0.0 69.6 jit_solution(5495652207003911730)
XLA Ops:
  0.0 0.8 %copy.9 = s32[1,32,2]{2,1,0:T(8,128)S(1)} copy(s32[1,32,2]{1,2,0:T(2,128)} %param.11) | data formatting | bytes 512 | tf_op args[4]
  0.8 0.6 reshape.13.send_ref
  1.4 27.2 %exchange.1 = (bf16[32,2,64,128]{3,2,1,0:T(8,128)(2,1)}, f32[8,128]{1,0:T(8,128)}) custom-call(s32[64]{0:T(128)} %reshape.13.send_ref, f32[256,128]{1,0:T(8,128)} %bitcast.6, bf16[64,32768]{1,0:T(8,128)(2,1)} %src_ref.1), custom_call_target="tpu_custom_call" | custom-call | tf_op jit(solution)/shard_map/exchange/pallas_call | solution.py:96
  28.6 21.0 %regrid.1 = (f32[64,8192]{1,0:T(8,128)}, f32[8,128]{1,0:T(8,128)}) custom-call(s32[384]{0:T(512)} %slot_ref.1, s32[384]{0:T(512)} %target_ref.1, bf16[64,64,128]{2,1,0:T(8,128)(2,1)} %bitcast.5, f32[64,128]{1,0:T(8,128)} %bitcast.7, bf16[384,128,128]{2,1,0:T(8,128)(2,1)} %weight_ref.1), custom_call_target="tpu_custom_call" | custom-call | tf_op jit(solution)/shard_map/regrid/pallas_call | solution.py:157
  49.6 16.1 %masses.1 = f32[8,128]{1,0:T(8,128)} custom-call(f32[8,128]{1,0:T(8,128)} %get-tuple-element.11.source_ref, f32[8,128]{1,0:T(8,128)} %get-tuple-element.12.target_ref), custom_call_target="tpu_custom_call" | custom-call | tf_op jit(solution)/shard_map/masses/pallas_call | solution.py:209
  65.8 0.7 slice_bitcast_fusion
  66.5 3.1 %broadcast_multiply_fusion = f32[64,8192]{1,0:T(8,128)} fusion(f32[64,8192]{1,0:T(8,128)} %get-tuple-element.10, f32[64]{0:T(128)S(1)} %slice_bitcast_fusion), kind=kLoop, calls=%fused_computation | loop fusion | flops 524288 | bytes 4194560 | tf_op jit(solution)/shard_map/mul | solution.py:232

commit v2 on v0

v2 whole, which is shorter than its diff:
```python
import functools

import jax
import jax.numpy as jnp
from jax import lax
from jax.experimental import pallas as pl
from jax.experimental.pallas import tpu as pltpu
from jax.sharding import PartitionSpec as P

MESH = pl.DeviceIdType.MESH
LANES = 128


def lanes_of(column):
    total = jnp.sum(column, axis=1, keepdims=True)
    rows = lax.broadcasted_iota(jnp.int32, column.shape, 0)
    lanes = lax.broadcasted_iota(jnp.int32, column.shape, 1)
    return jnp.sum(jnp.where(rows == lanes, total, 0.0), axis=0, keepdims=True)


def place(cols):
    me = lax.axis_index("row") * cols + lax.axis_index("col")
    return me


def greet(n, cols, me):
    barrier = pltpu.get_barrier_semaphore()

    def hello(step, carry):
        peer = lax.rem(me + step, n)
        pl.semaphore_signal(barrier, inc=1, device_id=(peer // cols, lax.rem(peer, cols)), device_id_type=MESH)
        return carry

    lax.fori_loop(1, n, hello, 0)
    return barrier


def exchange_kernel(
    n, cols, cuts, send_ref, slot_ref, target_ref, slots_ref, source_area_ref, target_area_ref, src_ref, weight_ref,
    inbound_ref, scale_ref,
    src, outbound, weights, asked, wanted, part, own, seen,
    load_sem, weight_sem, keep_sem, send_sem, recv_sem, ask_send, ask_recv, mass_send, mass_recv,
):
    me = place(cols)
    capacity, columns, block = outbound.shape[1:]
    pairs = weight_ref.shape[0]
    chunks = weight_sem.shape[0]
    chunk = pairs // chunks

    def load(index, carry):
        cells = pl.ds(pl.multiple_of(index * block, block), block)
        pltpu.make_async_copy(src_ref.at[:, cells], src.at[index], load_sem).start()
        return carry

    def fetch(index):
        piece = pl.ds(index * chunk, chunk)
        return pltpu.make_async_copy(weight_ref.at[piece], weights.at[piece], weight_sem.at[index])

    lax.fori_loop(0, src.shape[0], load, 0, unroll=8)
    barrier = greet(n, cols, me)
    pltpu.make_async_copy(src, src, load_sem).wait()
    for index in range(chunks):
        fetch(index).start()

    def gather(peer, carry):
        for slot in range(capacity):
            outbound[peer, slot] = src[jnp.maximum(send_ref[slot, peer], 0)]
        return carry

    lax.fori_loop(0, n, gather, 0)
    pl.semaphore_wait(barrier, n - 1)

    def to_peer(step, source, target, sent, received):
        peer = lax.rem(me + step, n)
        return pltpu.make_async_remote_copy(
            src_ref=source(peer),
            dst_ref=target,
            send_sem=sent.at[step],
            recv_sem=received.at[step],
            device_id=(peer // cols, lax.rem(peer, cols)),
            device_id_type=MESH,
        )

    def blocks(step):
        return to_peer(step, lambda peer: outbound.at[peer], inbound_ref.at[me], send_sem, recv_sem)

    def asks(step):
        return to_peer(step, lambda peer: wanted.at[peer], asked.at[step], ask_send, ask_recv)

    def masses(step):
        return to_peer(step, lambda peer: own, seen.at[step], mass_send, mass_recv)

    def start(copy, low, high):
        def one(step, carry):
            copy(step).start()
            return carry

        lax.fori_loop(low, high, one, 0)

    start(blocks, 1, cuts[0])
    keep = pltpu.make_async_copy(outbound.at[me], inbound_ref.at[me], keep_sem)
    keep.start()

    group = 8

    def fold(index, carry):
        for inner in range(group):
            j = index * group + inner
            area = target_area_ref[target_ref[j]]
            high = area.astype(jnp.bfloat16)
            rest = area - high.astype(jnp.float32)
            middle = rest.astype(jnp.bfloat16)
            low = (rest - middle.astype(jnp.float32)).astype(jnp.bfloat16)
            terms = jnp.concatenate([high, middle, low], axis=0)
            sums = lax.dot_general(terms, weights[j], (((1,), (1,)), ((), ())), preferred_element_type=jnp.float32)
            part[pl.ds(j, 1), :] = sums[0:1] + sums[1:2] + sums[2:3]
        return carry

    for index in range(chunks):
        fetch(index).wait()
        lax.fori_loop(index * chunk // group, (index + 1) * chunk // group, fold, 0)

    sublanes = wanted.shape[1]
    rows = lax.broadcasted_iota(jnp.int32, (n * sublanes, pairs), 0)
    peer_of, slot_of = rows // sublanes, rows % sublanes
    names = jnp.where(slot_of < capacity, peer_of * capacity + slot_of, -1)
    chosen = jnp.where(names == slots_ref[...], 1.0, 0.0)
    sums = jnp.dot(chosen, part[...], precision=lax.Precision.HIGHEST, preferred_element_type=jnp.float32)
    wanted[...] = sums.reshape(wanted.shape)

    start(asks, 1, n)
    start(blocks, cuts[0], cuts[1])

    def add(index, total):
        return total + src[index].astype(jnp.float32) * source_area_ref[pl.ds(index, 1), :]

    zero = jnp.zeros((columns, block), jnp.float32)
    source = lanes_of(lax.fori_loop(0, src.shape[0], add, zero, unroll=8))

    def weigh(peer, share, total):
        for slot in range(capacity):
            total = total + outbound[peer, slot].astype(jnp.float32) * share[slot : slot + 1]
        return total

    def arrived(step, total):
        asks(step).wait()
        return weigh(lax.rem(me + n - step, n), asked[step], total)

    target = lanes_of(lax.fori_loop(1, n, arrived, weigh(me, wanted[me], zero)))
    rows = lax.broadcasted_iota(jnp.int32, own.shape, 0)
    own[...] = jnp.where(rows == 0, source, target)
    start(masses, 1, n)
    start(blocks, cuts[1], n)

    def collect(step, total):
        masses(step).wait()
        return total + seen[step]

    total = lax.fori_loop(1, n, collect, own[...])
    ratio = jnp.broadcast_to(total[0:1] / total[1:2], (columns, block))
    diagonal = lax.broadcasted_iota(jnp.int32, ratio.shape, 0) == lax.broadcasted_iota(jnp.int32, ratio.shape, 1)
    scale_ref[...] = jnp.broadcast_to(jnp.sum(jnp.where(diagonal, ratio, 0.0), axis=1, keepdims=True), ratio.shape)
    keep.wait()

    def finish(step, carry):
        blocks(step).wait()
        return carry

    lax.fori_loop(1, n, finish, 0)


def exchange(n, cols, send_rows, pair_slot, pair_target, source_area, target_area, src_field, weights):
    columns, cells = src_field.shape
    block = source_area.shape[1]
    capacity = send_rows.shape[0]
    pairs = weights.shape[0]
    cuts = (max(n * 4 // 10, 1), max(n * 7 // 10, 1))
    vmem = pl.BlockSpec(memory_space=pltpu.VMEM)
    smem = pl.BlockSpec(memory_space=pltpu.SMEM)
    hbm = pl.BlockSpec(memory_space=pl.ANY)
    per_peer = pltpu.SemaphoreType.DMA((n,))
    return pl.pallas_call(
        functools.partial(exchange_kernel, n, cols, cuts),
        out_shape=(
            jax.ShapeDtypeStruct((n, capacity, columns, block), jnp.bfloat16),
            jax.ShapeDtypeStruct((columns, block), jnp.float32),
        ),
        in_specs=[smem, smem, smem, vmem, vmem, vmem, hbm, hbm],
        out_specs=(hbm, vmem),
        scratch_shapes=[
            pltpu.VMEM((cells // block, columns, block), jnp.bfloat16),
            pltpu.VMEM((n, capacity, columns, block), jnp.bfloat16),
            pltpu.VMEM(weights.shape, jnp.bfloat16),
            pltpu.VMEM((n, 8, block), jnp.float32),
            pltpu.VMEM((n, 8, block), jnp.float32),
            pltpu.VMEM((pairs, block), jnp.float32),
            pltpu.VMEM((8, block), jnp.float32),
            pltpu.VMEM((n, 8, block), jnp.float32),
            pltpu.SemaphoreType.DMA,
            pltpu.SemaphoreType.DMA((4,)),
            pltpu.SemaphoreType.DMA,
        ]
        + [per_peer] * 6,
        compiler_params=pltpu.CompilerParams(collective_id=0, has_side_effects=True),
        name="exchange",
    )(send_rows, pair_slot, pair_target, pair_slot.reshape(1, pairs), source_area, target_area, src_field, weights)


def regrid_kernel(lag, slot_ref, target_ref, inbound_ref, scale_ref, weight_ref, out_ref):
    step = pl.program_id(0)
    group, block = weight_ref.shape[:2]
    products = {}

    @pl.when(step == 0)
    def _():
        out_ref[...] = jnp.zeros_like(out_ref)

    def cells_of(target):
        return pl.ds(pl.multiple_of(target * block, block), block)

    for inner in range(group + lag):
        if inner < group:
            slot = slot_ref[step * group + inner]
            products[inner] = jnp.dot(inbound_ref[slot], weight_ref[inner], preferred_element_type=jnp.float32)
        if inner >= lag:
            cells = cells_of(target_ref[step * group + inner - lag])
            out_ref[:, cells] += products.pop(inner - lag)

    @pl.when(step == pl.num_programs(0) - 1)
    def _():
        def fix(index, carry):
            out_ref[:, cells_of(index)] = out_ref[:, cells_of(index)] * scale_ref[...]
            return carry

        lax.fori_loop(0, out_ref.shape[1] // block, fix, 0, unroll=8)


def regrid(inbound, scale, weights, pair_slot, pair_target, targets):
    slots, columns, block = inbound.shape
    pairs = weights.shape[0]
    group = next(g for g in (48, 32, 16, 8, 4, 2, 1) if pairs % g == 0)
    whole = lambda *shape: pl.BlockSpec(shape, lambda i, *_: (0,) * len(shape))
    return pl.pallas_call(
        functools.partial(regrid_kernel, 6),
        out_shape=jax.ShapeDtypeStruct((columns, targets * block), jnp.float32),
        grid_spec=pltpu.PrefetchScalarGridSpec(
            num_scalar_prefetch=2,
            grid=(pairs // group,),
            in_specs=[
                whole(slots, columns, block),
                whole(columns, block),
                pl.BlockSpec((group, block, block), lambda i, *_: (i, 0, 0)),
            ],
            out_specs=whole(columns, targets * block),
        ),
        name="regrid",
    )(pair_slot, pair_target, inbound, scale, weights)


def shards(n, cols, src_field, src_area, tgt_area, weights, send_index, pair_slot, pair_target):
    columns, cell_count = src_field.shape
    block = weights.shape[1]
    targets = tgt_area.shape[0] // block
    inbound, scale = exchange(
        n, cols, send_index[0].T, pair_slot, pair_target,
        src_area.reshape(-1, block), tgt_area.reshape(targets, 1, block), src_field, weights,
    )
    return regrid(inbound.reshape(-1, columns, block), scale, weights, pair_slot, pair_target, targets)


def solution(mesh):
    rows, cols = mesh.shape["row"], mesh.shape["col"]
    in_specs = (
        P(None, ("row", "col")),
        P(("row", "col")),
        P(("row", "col")),
        P(("row", "col"), None, None),
        P(("row", "col"), None, None),
        P(("row", "col")),
        P(("row", "col")),
    )
    out_specs = P(None, ("row", "col"))
    body = functools.partial(shards, rows * cols, cols)
    return jax.shard_map(body, mesh=mesh, in_specs=in_specs, out_specs=out_specs, check_vma=False)
```

time: 154 us -> 61.8 us (0.40)
  the two profiles are of different devices: /device:TPU:0 before, /device:TPU:15 now
where the time goes in v2:
time: 61.8 us; the launch traced here: 61.5 us
  Pallas kernels  60.2 us (97%)
  local copies, waits for them, and re-layouts  1.24 us (2%)
    pallas_call x1, Pallas kernels, exchange(): pl.pallas_call(functools.partial(exchange_kernel, n, cols, cuts), out_sha...  48.3 us
    pallas_call x1, Pallas kernels, regrid(): pl.pallas_call(functools.partial(regrid_kernel, 6), out_shape=jax.ShapeDt...  11.9 us
    reshape x1, local copies, waits for them, and re-layouts, exchange(): pair_slot.reshape(1, pairs)  1.24 us

profile of v2, /device:TPU:15, one launch (start us, length us, event | category | flops | bytes accessed | tf_op | source)
XLA Modules:
  0.0 61.5 jit_solution(6569964568566497867)
XLA Ops:
  0.0 1.2 %reshape.12.slots_ref = s32[1,384]{1,0:T(1,128)} reshape(s32[384]{0:T(512)} %slot_ref.3) | data formatting | bytes 3072 | tf_op jit(solution)/shard_map/reshape | solution.py:206
  1.2 48.3 %exchange.1 = (bf16[32,2,64,128]{3,2,1,0:T(8,128)(2,1)}, f32[64,128]{1,0:T(8,128)}) custom-call(s32[2,32]{1,0:T(2,128)} %bitcast.9, s32[384]{0:T(512)} %slot_ref.3, s32[384]{0:T(512)} %target_ref.3, s32[1,384]{1,0:T(1,128)} %reshape.12.slots_ref, f32[256,128]{1,0:T(8,128)} %bitcast.7, f32[64,1,128]{2,1,0:T(1,128)} %bitcast.8, bf16[64,32768]{1,0:T(8,128)(2,1)} %src_ref.1, ...), custom_call_target="tpu_custom_call" | custom-call | tf_op jit(solution)/shard_map/exchange/pallas_call | solution.py:182
  49.6 11.9 %regrid.1 = f32[64,8192]{1,0:T(8,128)} custom-call(s32[384]{0:T(512)} %slot_ref.3, s32[384]{0:T(512)} %target_ref.3, bf16[64,64,128]{2,1,0:T(8,128)(2,1)} %bitcast.6, f32[64,128]{1,0:T(8,128)} %get-tuple-element.8.scale_ref, bf16[384,128,128]{2,1,0:T(8,128)(2,1)} %weight_ref.3), custom_call_target="tpu_custom_call" | custom-call | tf_op jit(solution)/shard_map/regrid/pallas_call | solution.py:243

commit v3 on v2

--- a/solution.py
+++ b/solution.py
@@ -35,11 +35,18 @@
     return barrier
 
 
+def split(value):
+    high = value.astype(jnp.bfloat16)
+    rest = value - high.astype(jnp.float32)
+    middle = rest.astype(jnp.bfloat16)
+    return high, middle, (rest - middle.astype(jnp.float32)).astype(jnp.bfloat16)
+
+
 def exchange_kernel(
-    n, cols, cuts, send_ref, slot_ref, target_ref, slots_ref, source_area_ref, target_area_ref, src_ref, weight_ref,
+    n, cols, send_ref, slot_ref, target_ref, slots_ref, source_area_ref, target_area_ref, src_ref, weight_ref,
     inbound_ref, scale_ref,
-    src, outbound, weights, asked, wanted, part, own, seen,
-    load_sem, weight_sem, keep_sem, send_sem, recv_sem, ask_send, ask_recv, mass_send, mass_recv,
+    src, outbound, weights, part, shares, own, seen,
+    load_sem, weight_sem, keep_sem, send_sem, recv_sem, mass_send, mass_recv,
 ):
     me = place(cols)
     capacity, columns, block = outbound.shape[1:]
@@ -70,66 +77,53 @@
     lax.fori_loop(0, n, gather, 0)
     pl.semaphore_wait(barrier, n - 1)
 
-    def to_peer(step, source, target, sent, received):
+    def blocks(step):
         peer = lax.rem(me + step, n)
         return pltpu.make_async_remote_copy(
-            src_ref=source(peer),
-            dst_ref=target,
-            send_sem=sent.at[step],
-            recv_sem=received.at[step],
+            src_ref=outbound.at[peer],
+            dst_ref=inbound_ref.at[me],
+            send_sem=send_sem.at[step],
+            recv_sem=recv_sem.at[step],
             device_id=(peer // cols, lax.rem(peer, cols)),
             device_id_type=MESH,
         )
 
-    def blocks(step):
-        return to_peer(step, lambda peer: outbound.at[peer], inbound_ref.at[me], send_sem, recv_sem)
-
-    def asks(step):
-        return to_peer(step, lambda peer: wanted.at[peer], asked.at[step], ask_send, ask_recv)
-
-    def masses(step):
-        return to_peer(step, lambda peer: own, seen.at[step], mass_send, mass_recv)
-
-    def start(copy, low, high):
-        def one(step, carry):
-            copy(step).start()
-            return carry
-
-        lax.fori_loop(low, high, one, 0)
-
-    start(blocks, 1, cuts[0])
+    def send(step, carry):
+        blocks(step).start()
+        return carry
+
+    lax.fori_loop(1, n, send, 0)
     keep = pltpu.make_async_copy(outbound.at[me], inbound_ref.at[me], keep_sem)
     keep.start()
 
-    group = 8
+    group = max(g for g in (16, 8, 4, 2, 1) if chunk % g == 0)
+    row = lax.broadcasted_iota(jnp.int32, (group, block), 0)
 
     def fold(index, carry):
-        for inner in range(group):
-            j = index * group + inner
-            area = target_area_ref[target_ref[j]]
-            high = area.astype(jnp.bfloat16)
-            rest = area - high.astype(jnp.float32)
-            middle = rest.astype(jnp.bfloat16)
-            low = (rest - middle.astype(jnp.float32)).astype(jnp.bfloat16)
-            terms = jnp.concatenate([high, middle, low], axis=0)
-            sums = lax.dot_general(terms, weights[j], (((1,), (1,)), ((), ())), preferred_element_type=jnp.float32)
-            part[pl.ds(j, 1), :] = sums[0:1] + sums[1:2] + sums[2:3]
+        first = index * group
+        area = jnp.concatenate([target_area_ref[target_ref[first + inner]] for inner in range(group)], axis=0)
+        tiles = weights[pl.ds(first, group)].reshape(group * block, block)
+        terms = jnp.concatenate(split(area), axis=0)
+        sums = lax.dot_general(terms, tiles, (((1,), (1,)), ((), ())), preferred_element_type=jnp.float32)
+        sums = sums[:group] + sums[group : 2 * group] + sums[2 * group :]
+        own_sums = sums[:, :block]
+        for inner in range(1, group):
+            own_sums = jnp.where(row == inner, sums[:, inner * block : (inner + 1) * block], own_sums)
+        part[pl.ds(pl.multiple_of(first, group), group), :] = own_sums
         return carry
 
     for index in range(chunks):
         fetch(index).wait()
         lax.fori_loop(index * chunk // group, (index + 1) * chunk // group, fold, 0)
 
-    sublanes = wanted.shape[1]
+    sublanes = shares.shape[1]
     rows = lax.broadcasted_iota(jnp.int32, (n * sublanes, pairs), 0)
     peer_of, slot_of = rows // sublanes, rows % sublanes
     names = jnp.where(slot_of < capacity, peer_of * capacity + slot_of, -1)
-    chosen = jnp.where(names == slots_ref[...], 1.0, 0.0)
-    sums = jnp.dot(chosen, part[...], precision=lax.Precision.HIGHEST, preferred_element_type=jnp.float32)
-    wanted[...] = sums.reshape(wanted.shape)
-
-    start(asks, 1, n)
-    start(blocks, cuts[0], cuts[1])
+    chosen = jnp.where(names == slots_ref[...].reshape(1, pairs), 1.0, 0.0).astype(jnp.bfloat16)
+    sums = jnp.dot(chosen, jnp.concatenate(split(part[...]), axis=1), preferred_element_type=jnp.float32)
+    sums = sums[:, :block] + sums[:, block : 2 * block] + sums[:, 2 * block :]
+    shares[...] = sums.reshape(shares.shape)
 
     def add(index, total):
         return total + src[index].astype(jnp.float32) * source_area_ref[pl.ds(index, 1), :]
@@ -137,33 +131,47 @@
     zero = jnp.zeros((columns, block), jnp.float32)
     source = lanes_of(lax.fori_loop(0, src.shape[0], add, zero, unroll=8))
 
-    def weigh(peer, share, total):
+    def weigh(peer, held, total):
+        share = shares[peer]
         for slot in range(capacity):
-            total = total + outbound[peer, slot].astype(jnp.float32) * share[slot : slot + 1]
+            total = total + held[peer, slot].astype(jnp.float32) * share[slot : slot + 1]
         return total
 
     def arrived(step, total):
-        asks(step).wait()
-        return weigh(lax.rem(me + n - step, n), asked[step], total)
-
-    target = lanes_of(lax.fori_loop(1, n, arrived, weigh(me, wanted[me], zero)))
-    rows = lax.broadcasted_iota(jnp.int32, own.shape, 0)
-    own[...] = jnp.where(rows == 0, source, target)
-    start(masses, 1, n)
-    start(blocks, cuts[1], n)
-
-    def collect(step, total):
-        masses(step).wait()
-        return total + seen[step]
-
-    total = lax.fori_loop(1, n, collect, own[...])
+        blocks(step).wait_recv()
+        return weigh(lax.rem(me + n - step, n), inbound_ref, total)
+
+    target = lanes_of(lax.fori_loop(1, n, arrived, weigh(me, outbound, zero)))
+    rows = lax.broadcasted_iota(jnp.int32, own.shape[1:], 0)
+    total = jnp.where(rows == 0, source, target)
+    row, col = lax.axis_index("row"), lax.axis_index("col")
+    for stage, size in enumerate((cols, n // cols)):
+        own[stage] = total
+
+        def masses(step):
+            peer = (row, lax.rem(col + step, size)) if stage == 0 else (lax.rem(row + step, size), col)
+            return pltpu.make_async_remote_copy(
+                src_ref=own.at[stage],
+                dst_ref=seen.at[stage, step],
+                send_sem=mass_send.at[stage, step],
+                recv_sem=mass_recv.at[stage, step],
+                device_id=peer,
+                device_id_type=MESH,
+            )
+
+        for step in range(1, size):
+            masses(step).start()
+        for step in range(1, size):
+            masses(step).wait()
+            total = total + seen[stage, step]
+
     ratio = jnp.broadcast_to(total[0:1] / total[1:2], (columns, block))
     diagonal = lax.broadcasted_iota(jnp.int32, ratio.shape, 0) == lax.broadcasted_iota(jnp.int32, ratio.shape, 1)
     scale_ref[...] = jnp.broadcast_to(jnp.sum(jnp.where(diagonal, ratio, 0.0), axis=1, keepdims=True), ratio.shape)
     keep.wait()
 
     def finish(step, carry):
-        blocks(step).wait()
+        blocks(step).wait_send()
         return carry
 
     lax.fori_loop(1, n, finish, 0)
@@ -174,36 +182,35 @@
     block = source_area.shape[1]
     capacity = send_rows.shape[0]
     pairs = weights.shape[0]
-    cuts = (max(n * 4 // 10, 1), max(n * 7 // 10, 1))
     vmem = pl.BlockSpec(memory_space=pltpu.VMEM)
     smem = pl.BlockSpec(memory_space=pltpu.SMEM)
     hbm = pl.BlockSpec(memory_space=pl.ANY)
-    per_peer = pltpu.SemaphoreType.DMA((n,))
+    longest = max(cols, n // cols)
     return pl.pallas_call(
-        functools.partial(exchange_kernel, n, cols, cuts),
+        functools.partial(exchange_kernel, n, cols),
         out_shape=(
             jax.ShapeDtypeStruct((n, capacity, columns, block), jnp.bfloat16),
             jax.ShapeDtypeStruct((columns, block), jnp.float32),
         ),
         in_specs=[smem, smem, smem, vmem, vmem, vmem, hbm, hbm],
-        out_specs=(hbm, vmem),
+        out_specs=(vmem, vmem),
         scratch_shapes=[
             pltpu.VMEM((cells // block, columns, block), jnp.bfloat16),
             pltpu.VMEM((n, capacity, columns, block), jnp.bfloat16),
             pltpu.VMEM(weights.shape, jnp.bfloat16),
+            pltpu.VMEM((pairs, block), jnp.float32),
             pltpu.VMEM((n, 8, block), jnp.float32),
-            pltpu.VMEM((n, 8, block), jnp.float32),
-            pltpu.VMEM((pairs, block), jnp.float32),
-            pltpu.VMEM((8, block), jnp.float32),
-            pltpu.VMEM((n, 8, block), jnp.float32),
+            pltpu.VMEM((2, 8, block), jnp.float32),
+            pltpu.VMEM((2, longest, 8, block), jnp.float32),
             pltpu.SemaphoreType.DMA,
             pltpu.SemaphoreType.DMA((4,)),
             pltpu.SemaphoreType.DMA,
         ]
-        + [per_peer] * 6,
+        + [pltpu.SemaphoreType.DMA((n,))] * 2
+        + [pltpu.SemaphoreType.DMA((2, longest))] * 2,
         compiler_params=pltpu.CompilerParams(collective_id=0, has_side_effects=True),
         name="exchange",
-    )(send_rows, pair_slot, pair_target, pair_slot.reshape(1, pairs), source_area, target_area, src_field, weights)
+    )(send_rows, pair_slot, pair_target, pair_slot, source_area, target_area, src_field, weights)
 
 
 def regrid_kernel(lag, slot_ref, target_ref, inbound_ref, scale_ref, weight_ref, out_ref):
@@ -238,7 +245,7 @@
 def regrid(inbound, scale, weights, pair_slot, pair_target, targets):
     slots, columns, block = inbound.shape
     pairs = weights.shape[0]
-    group = next(g for g in (48, 32, 16, 8, 4, 2, 1) if pairs % g == 0)
+    group = next(g for g in (96, 64, 48, 32, 16, 8, 4, 2, 1) if pairs % g == 0)
     whole = lambda *shape: pl.BlockSpec(shape, lambda i, *_: (0,) * len(shape))
     return pl.pallas_call(
         functools.partial(regrid_kernel, 6),

time: 61.8 us -> 53.8 us (0.87)
  the two profiles are of different devices: /device:TPU:15 before, /device:TPU:0 now
where the time goes in v3:
time: 53.8 us; the launch traced here: 53.5 us
  Pallas kernels  53.5 us (99%)
    pallas_call x1, Pallas kernels, exchange(): pl.pallas_call(functools.partial(exchange_kernel, n, cols), out_shape=(ja...  43.4 us
    pallas_call x1, Pallas kernels, regrid(): pl.pallas_call(functools.partial(regrid_kernel, 6), out_shape=jax.ShapeDt...  10.1 us

profile of v3, /device:TPU:0, one launch (start us, length us, event | category | flops | bytes accessed | tf_op | source)
XLA Modules:
  0.0 53.5 jit_solution(2495174422324626257)
XLA Ops:
  0.0 43.4 %exchange.1 = (bf16[32,2,64,128]{3,2,1,0:T(8,128)(2,1)}, f32[64,128]{1,0:T(8,128)}) custom-call(s32[2,32]{1,0:T(2,128)} %bitcast.9, s32[384]{0:T(512)} %slot_ref.3, s32[384]{0:T(512)} %target_ref.3, s32[384]{0:T(512)} %slot_ref.3, f32[256,128]{1,0:T(8,128)} %bitcast.7, f32[64,1,128]{2,1,0:T(1,128)} %bitcast.8, bf16[64,32768]{1,0:T(8,128)(2,1)} %src_ref.1, ...), custom_call_target="tpu_custom_call" | custom-call | tf_op jit(solution)/shard_map/exchange/pallas_call | solution.py:189
  43.4 10.1 %regrid.1 = f32[64,8192]{1,0:T(8,128)} custom-call(s32[384]{0:T(512)} %slot_ref.3, s32[384]{0:T(512)} %target_ref.3, bf16[64,64,128]{2,1,0:T(8,128)(2,1)} %bitcast.6, f32[64,128]{1,0:T(8,128)} %get-tuple-element.8.scale_ref, bf16[384,128,128]{2,1,0:T(8,128)(2,1)} %weight_ref.3), custom_call_target="tpu_custom_call" | custom-call | tf_op jit(solution)/shard_map/regrid/pallas_call | solution.py:250

commit v4 on v3

--- a/solution.py
+++ b/solution.py
@@ -1,4 +1,5 @@
 import functools
+import math
 
 import jax
 import jax.numpy as jnp
@@ -77,27 +78,28 @@
     lax.fori_loop(0, n, gather, 0)
     pl.semaphore_wait(barrier, n - 1)
 
+    row, col = lax.axis_index("row"), lax.axis_index("col")
+    steps = order(n // cols, cols)
+
     def blocks(step):
-        peer = lax.rem(me + step, n)
+        down, across = steps[step]
+        to_row, to_col = lax.rem(row + down, n // cols), lax.rem(col + across, cols)
         return pltpu.make_async_remote_copy(
-            src_ref=outbound.at[peer],
+            src_ref=outbound.at[to_row * cols + to_col],
             dst_ref=inbound_ref.at[me],
             send_sem=send_sem.at[step],
             recv_sem=recv_sem.at[step],
-            device_id=(peer // cols, lax.rem(peer, cols)),
+            device_id=(to_row, to_col),
             device_id_type=MESH,
         )
 
-    def send(step, carry):
+    for step in range(n - 1):
         blocks(step).start()
-        return carry
-
-    lax.fori_loop(1, n, send, 0)
     keep = pltpu.make_async_copy(outbound.at[me], inbound_ref.at[me], keep_sem)
     keep.start()
 
     group = max(g for g in (16, 8, 4, 2, 1) if chunk % g == 0)
-    row = lax.broadcasted_iota(jnp.int32, (group, block), 0)
+    place_of = lax.broadcasted_iota(jnp.int32, (group, block), 0)
 
     def fold(index, carry):
         first = index * group
@@ -108,7 +110,7 @@
         sums = sums[:group] + sums[group : 2 * group] + sums[2 * group :]
         own_sums = sums[:, :block]
         for inner in range(1, group):
-            own_sums = jnp.where(row == inner, sums[:, inner * block : (inner + 1) * block], own_sums)
+            own_sums = jnp.where(place_of == inner, sums[:, inner * block : (inner + 1) * block], own_sums)
         part[pl.ds(pl.multiple_of(first, group), group), :] = own_sums
         return carry
 
@@ -137,44 +139,48 @@
             total = total + held[peer, slot].astype(jnp.float32) * share[slot : slot + 1]
         return total
 
-    def arrived(step, total):
+    total = weigh(me, outbound, zero)
+    for step, (down, across) in enumerate(steps):
         blocks(step).wait_recv()
-        return weigh(lax.rem(me + n - step, n), inbound_ref, total)
-
-    target = lanes_of(lax.fori_loop(1, n, arrived, weigh(me, outbound, zero)))
-    rows = lax.broadcasted_iota(jnp.int32, own.shape[1:], 0)
-    total = jnp.where(rows == 0, source, target)
-    row, col = lax.axis_index("row"), lax.axis_index("col")
-    for stage, size in enumerate((cols, n // cols)):
-        own[stage] = total
-
-        def masses(step):
-            peer = (row, lax.rem(col + step, size)) if stage == 0 else (lax.rem(row + step, size), col)
-            return pltpu.make_async_remote_copy(
-                src_ref=own.at[stage],
-                dst_ref=seen.at[stage, step],
-                send_sem=mass_send.at[stage, step],
-                recv_sem=mass_recv.at[stage, step],
-                device_id=peer,
-                device_id_type=MESH,
-            )
-
-        for step in range(1, size):
-            masses(step).start()
-        for step in range(1, size):
-            masses(step).wait()
-            total = total + seen[stage, step]
-
+        from_row, from_col = lax.rem(row + n // cols - down, n // cols), lax.rem(col + cols - across, cols)
+        total = weigh(from_row * cols + from_col, inbound_ref, total)
+    rows = lax.broadcasted_iota(jnp.int32, own.shape, 0)
+    own[...] = jnp.where(rows == 0, source, lanes_of(total))
+
+    def masses(step):
+        peer = lax.rem(me + step, n)
+        return pltpu.make_async_remote_copy(
+            src_ref=own,
+            dst_ref=seen.at[step],
+            send_sem=mass_send.at[step],
+            recv_sem=mass_recv.at[step],
+            device_id=(peer // cols, lax.rem(peer, cols)),
+            device_id_type=MESH,
+        )
+
+    def tell(step, carry):
+        masses(step).start()
+        return carry
+
+    def collect(step, total):
+        masses(step).wait()
+        return total + seen[step]
+
+    lax.fori_loop(1, n, tell, 0)
+    total = lax.fori_loop(1, n, collect, own[...])
     ratio = jnp.broadcast_to(total[0:1] / total[1:2], (columns, block))
     diagonal = lax.broadcasted_iota(jnp.int32, ratio.shape, 0) == lax.broadcasted_iota(jnp.int32, ratio.shape, 1)
     scale_ref[...] = jnp.broadcast_to(jnp.sum(jnp.where(diagonal, ratio, 0.0), axis=1, keepdims=True), ratio.shape)
     keep.wait()
 
-    def finish(step, carry):
+    for step in range(n - 1):
         blocks(step).wait_send()
-        return carry
-
-    lax.fori_loop(1, n, finish, 0)
+
+
+def order(rows, cols):
+    count = rows * cols
+    stride = next(k for k in (13, 11, 9, 7, 5, 3, 1) if math.gcd(k, count) == 1)
+    return [divmod(stride * step % count, cols) for step in range(1, count)]
 
 
 def exchange(n, cols, send_rows, pair_slot, pair_target, source_area, target_area, src_field, weights):
@@ -185,7 +191,6 @@
     vmem = pl.BlockSpec(memory_space=pltpu.VMEM)
     smem = pl.BlockSpec(memory_space=pltpu.SMEM)
     hbm = pl.BlockSpec(memory_space=pl.ANY)
-    longest = max(cols, n // cols)
     return pl.pallas_call(
         functools.partial(exchange_kernel, n, cols),
         out_shape=(
@@ -200,14 +205,13 @@
             pltpu.VMEM(weights.shape, jnp.bfloat16),
             pltpu.VMEM((pairs, block), jnp.float32),
             pltpu.VMEM((n, 8, block), jnp.float32),
-            pltpu.VMEM((2, 8, block), jnp.float32),
-            pltpu.VMEM((2, longest, 8, block), jnp.float32),
+            pltpu.VMEM((8, block), jnp.float32),
+            pltpu.VMEM((n, 8, block), jnp.float32),
             pltpu.SemaphoreType.DMA,
             pltpu.SemaphoreType.DMA((4,)),
             pltpu.SemaphoreType.DMA,
         ]
-        + [pltpu.SemaphoreType.DMA((n,))] * 2
-        + [pltpu.SemaphoreType.DMA((2, longest))] * 2,
+        + [pltpu.SemaphoreType.DMA((n,))] * 4,
         compiler_params=pltpu.CompilerParams(collective_id=0, has_side_effects=True),
         name="exchange",
     )(send_rows, pair_slot, pair_target, pair_slot, source_area, target_area, src_field, weights)
@@ -245,7 +249,7 @@
 def regrid(inbound, scale, weights, pair_slot, pair_target, targets):
     slots, columns, block = inbound.shape
     pairs = weights.shape[0]
-    group = next(g for g in (96, 64, 48, 32, 16, 8, 4, 2, 1) if pairs % g == 0)
+    group = next(g for g in (192, 96, 64, 48, 32, 16, 8, 4, 2, 1) if pairs % g == 0)
     whole = lambda *shape: pl.BlockSpec(shape, lambda i, *_: (0,) * len(shape))
     return pl.pallas_call(
         functools.partial(regrid_kernel, 6),

time: 53.8 us -> 49.8 us (0.926)
  Pallas kernels: 53.5 us -> 49.6 us
    pallas_call x1, Pallas kernels: 43.4 us -> 39.9 us  [exchange(): pl.pallas_call(functools.partial(exchange_kernel, n, cols), out_shape=(ja...]
where the time goes in v4:
time: 49.8 us; the launch traced here: 49.6 us
  Pallas kernels  49.6 us (100%)
    pallas_call x1, Pallas kernels, exchange(): pl.pallas_call(functools.partial(exchange_kernel, n, cols), out_shape=(ja...  39.9 us
    pallas_call x1, Pallas kernels, regrid(): pl.pallas_call(functools.partial(regrid_kernel, 6), out_shape=jax.ShapeDt...  9.68 us

profile of v4, /device:TPU:0, one launch (start us, length us, event | category | flops | bytes accessed | tf_op | source)
XLA Modules:
  0.0 49.6 jit_solution(10911737222596736438)
XLA Ops:
  0.0 39.9 %exchange.1 = (bf16[32,2,64,128]{3,2,1,0:T(8,128)(2,1)}, f32[64,128]{1,0:T(8,128)}) custom-call(s32[2,32]{1,0:T(2,128)} %bitcast.9, s32[384]{0:T(512)} %slot_ref.3, s32[384]{0:T(512)} %target_ref.3, s32[384]{0:T(512)} %slot_ref.3, f32[256,128]{1,0:T(8,128)} %bitcast.7, f32[64,1,128]{2,1,0:T(1,128)} %bitcast.8, bf16[64,32768]{1,0:T(8,128)(2,1)} %src_ref.1, ...), custom_call_target="tpu_custom_call" | custom-call | tf_op jit(solution)/shard_map/exchange/pallas_call | solution.py:194
  39.9 9.7 %regrid.1 = f32[64,8192]{1,0:T(8,128)} custom-call(s32[384]{0:T(512)} %slot_ref.3, s32[384]{0:T(512)} %target_ref.3, bf16[64,64,128]{2,1,0:T(8,128)(2,1)} %bitcast.6, f32[64,128]{1,0:T(8,128)} %get-tuple-element.8.scale_ref, bf16[384,128,128]{2,1,0:T(8,128)(2,1)} %weight_ref.3), custom_call_target="tpu_custom_call" | custom-call | tf_op jit(solution)/shard_map/regrid/pallas_call | solution.py:254
